TPU v7x, 8 devices: a whole 2x2x1 slice. The times are simulated.
8 devices in a mesh: dp: 1 (over z), dcp: 8 (over y, x, core).
Axes of the slice: x: 2, y: 2, z: 1, core: 2. Of those that a mesh axis runs over, the one named last changes fastest.
Arguments:
- q_abs: bfloat16 [128, 128, 576], P('dp', 'dcp')
- latent_cache: bfloat16 [128, 4, 8, 256, 576], P('dp', None, 'dcp')
- ctx_len: int32 [128], P('dp')
Outputs:
- output: bfloat16 [128, 128, 512], P(('dp', 'dcp'))
All inputs are finite; a program needn't handle non-finite values.
Results may differ from a plain program's by a relative error of at most 0.00644688.
Values are sent between devices in bfloat16 or wider.
A program may use at most 1 GiB of HBM per device.

v0:
```python
import jax
import jax.numpy as jnp
from jax import lax
from jax.sharding import PartitionSpec as P

ROPE_DIM = 64
QK_DIM = 192


def solution(mesh):
    group_size = mesh.shape['dcp']

    def local_step(q_blk, cache_blk, len_blk):
        batch_rows = q_blk.shape[0]
        num_pages = cache_blk.shape[1]
        page_len = cache_blk.shape[3]
        latent_dim = q_blk.shape[2] - ROPE_DIM
        out_rows = batch_rows // group_size
        dev_index = lax.axis_index('dcp')
        q_full = lax.all_gather(q_blk, 'dcp', axis=1, tiled=True)
        cache_own = cache_blk[:, :, 0]
        scores = jnp.einsum('bhw,bjtw->bhjt', q_full, cache_own, preferred_element_type=jnp.float32) * (QK_DIM ** -0.5)
        positions = (jnp.arange(num_pages)[:, None] * group_size + dev_index) * page_len + jnp.arange(page_len)[None, :]
        is_valid = positions[None] < len_blk[:, None, None]
        scores = jnp.where(is_valid[:, None], scores, -1e30)
        row_max = jnp.max(scores, axis=(2, 3))
        weights_exp = jnp.exp(scores - row_max[:, :, None, None])
        denom_sum = jnp.sum(weights_exp, axis=(2, 3))
        pv_sum = jnp.einsum('bhjt,bjtw->bhw', weights_exp.astype(jnp.bfloat16), cache_own, preferred_element_type=jnp.float32)
        part_out = (pv_sum[..., :latent_dim] / denom_sum[..., None]).astype(jnp.bfloat16)
        part_lse = row_max + jnp.log(denom_sum)
        recv_out = lax.all_to_all(part_out, 'dcp', 0, 0, tiled=True).reshape(group_size, out_rows, part_out.shape[1], latent_dim)
        recv_lse = lax.all_to_all(part_lse, 'dcp', 0, 0, tiled=True).reshape(group_size, out_rows, part_lse.shape[1])
        total_lse = jax.nn.logsumexp(recv_lse, axis=0)
        merge_weights = jnp.exp(recv_lse - total_lse[None])
        merged = jnp.sum(merge_weights[..., None] * recv_out.astype(jnp.float32), axis=0)
        return merged.astype(jnp.bfloat16)

    return jax.shard_map(local_step, mesh=mesh, in_specs=(P('dp', 'dcp', None), P('dp', None, 'dcp', None, None), P('dp')), out_specs=P(('dp', 'dcp'), None, None), check_vma=False)
```

profile of v0, /device:TPU:0, one launch (start us, length us, event | category | flops | bytes accessed | tf_op | source)
XLA Modules:
  0.0 524.5 jit_solution(17279507542600023722)
XLA Ops:
  6.5 0.0 all-gather.2.cloned.1.call-start
  6.5 4.9 copy.4
  11.5 0.0 all-gather.2.cloned.1.call-update
  11.5 0.1 iota_add_fusion
  11.6 0.9 broadcast_compare_fusion
  12.4 103.6 %all-gather.2.cloned.1.call-done = bf16[128,128,576]{2,1,0:T(8,128)(2,1)} async-done(((bf16[128,16,576]{2,1,0:T(8,128)(2,1)}), bf16[128,128,576]{2,1,0:T(8,128)(2,1)}) %all-gather.2.cloned.1.call-update) | async-done | bytes 18874384 | tf_op jit(solution)/shard_map/all_gather | solution.py:20
  116.0 75.5 %fusion.4 = (f32[128,128]{1,0:T(8,128)S(1)}, f32[128,128,4,256]{3,1,2,0:T(8,128)}) fusion(pred[128,4,256]{2,1,0:T(4,128)(4,1)S(1)} %broadcast_compare_fusion, bf16[128,4,1,256,576]{3,4,2,1,0:T(8,128)(2,1)} %param.4, bf16[128,128,576]{2,1,0:T(8,128)(2,1)} %all-gather.2.cloned.1.call-done), kind=kOutput, calls=%fused_computation.6 | convolution fusion | flops 19377668096 | bytes 237174784 | tf_op jit(solution)/shard_map/bhw,bjtw->bhjt/dot_general | solution.py:22
  191.5 21.5 %fusion.6 = f32[128,128]{1,0:T(8,128)S(1)} fusion(f32[128,128,4,256]{3,1,2,0:T(8,128)} %get-tuple-element.6, f32[128,128]{1,0:T(8,128)S(1)} %get-tuple-element.5, pred[128,4,256]{2,1,0:T(4,128)(4,1)S(1)} %broadcast_compare_fusion), kind=kLoop, calls=%fused_computation.8 | loop fusion | flops 67092480 | bytes 67371008 | tf_op jit(solution)/shard_map/reduce_sum | solution.py:28
  213.0 86.7 %fusion.15 = f32[128,128,576]{2,1,0:T(8,128)} fusion(bf16[128,4,1,256,576]{3,4,2,1,0:T(8,128)(2,1)} %param.4, f32[128,128,4,256]{3,1,2,0:T(8,128)} %get-tuple-element.6, f32[128,128]{1,0:T(8,128)S(1)} %get-tuple-element.5, pred[128,4,256]{2,1,0:T(4,128)(4,1)S(1)} %broadcast_compare_fusion), kind=kOutput, calls=%fused_computation.18 | convolution fusion | flops 19394461696 | bytes 256049152 | tf_op jit(solution)/shard_map/bhjt,bjtw->bhw/dot_general | solution.py:29
  299.7 0.6 log_add_fusion
  300.4 2.1 all-to-all-start
  302.5 17.7 %fusion.8 = bf16[128,128,512]{2,1,0:T(8,128)(2,1)} fusion(f32[128,128,576]{2,1,0:T(8,128)} %fusion.15, f32[128,128]{1,0:T(8,128)S(1)} %fusion.6), kind=kLoop, calls=%fused_computation.10 | loop fusion | flops 16777216 | bytes 50397184 | tf_op jit(solution)/shard_map/convert_element_type | solution.py:30
  320.2 0.0 all-to-all-done
  320.2 4.5 all-to-all-start.1
  324.8 183.8 %all-to-all-done.1 = bf16[128,128,512]{2,1,0:T(8,128)(2,1)} async-done(((bf16[128,128,512]{2,1,0:T(8,128)(2,1)}), bf16[128,128,512]{2,1,0:T(8,128)(2,1)}, u32[]{:S(2)}, u32[]{:S(2)}) %all-to-all-start.1) | async-done | bytes 16777248 | tf_op jit(solution)/shard_map/all_to_all | solution.py:32
  508.6 9.0 %fusion.9 = bf16[16,128,512]{2,1,0:T(8,128)(2,1)} fusion(bf16[8,16,128,512]{3,2,1,0:T(8,128)(2,1)} %bitcast.8, f32[8,16,128]{2,1,0:T(8,128)S(1)} %subtract_exponential_fusion.1), kind=kLoop, calls=%fused_computation.12 | loop fusion | flops 24117248 | bytes 18939904 | tf_op jit(solution)/shard_map/reduce_sum | solution.py:36
  (6 shorter events, 0.1 us)
Async XLA Ops:
  6.5 109.5 %all-gather.2.cloned.1.call-start = ((), (), s32[]{:S(2)}) async-start(), calls=%async_computation.2 | async-start | bytes 23592960 | tf_op jit(solution)/shard_map/all_gather | solution.py:20
  300.4 19.8 %all-to-all-start = ((f32[8,16,128]{2,1,0:T(8,128)}), f32[8,16,128]{2,1,0:T(8,128)S(1)}, u32[]{:S(2)}, u32[]{:S(2)}) async-start(f32[8,16,128]{2,1,0:T(8,128)} %bitcast.3), calls=%async_computation | async-start | bytes 131072 | tf_op jit(solution)/shard_map/all_to_all | solution.py:33
  320.2 188.4 %all-to-all-start.1 = ((bf16[128,128,512]{2,1,0:T(8,128)(2,1)}), bf16[128,128,512]{2,1,0:T(8,128)(2,1)}, u32[]{:S(2)}, u32[]{:S(2)}) async-start(bf16[128,128,512]{2,1,0:T(8,128)(2,1)} %fusion.8), calls=%async_computation.1 | async-start | bytes 33554432 | tf_op jit(solution)/shard_map/all_to_all | solution.py:32
Sparse Core Ops, SparseCore 0:
  11.6 104.3 all-gather.1
where the time goes:
time: 525 us; the launch traced here: 524 us
  waiting for transfers between devices  287 us (55%)
  matrix products  162 us (31%)
  other arithmetic  49.9 us (10%)
  between operations  13.5 us (3%)
  starting transfers between devices  6.58 us (1%)
    all_to_all x1, waiting for transfers between devices, local_step(): lax.all_to_all(part_out, 'dcp', 0, 0, tiled=True)  184 us
    all_gather x1, waiting for transfers between devices, local_step(): q_full = lax.all_gather(q_blk, 'dcp', axis=1, tiled=True)  104 us
    dot_general x1, matrix products, local_step(): jnp.einsum('bhjt,bjtw->bhw', weights_exp.astype(jnp.bfloat16), cache_own,...  86.7 us
    dot_general x1, matrix products, local_step(): jnp.einsum('bhw,bjtw->bhjt', q_full, cache_own, preferred_element_type=jn...  75.5 us
    reduce_sum x1, other arithmetic, local_step(): denom_sum = jnp.sum(weights_exp, axis=(2, 3))  21.5 us
    convert_element_type x1, other arithmetic, local_step(): (pv_sum[..., :latent_dim] / denom_sum[..., None]).astype(jnp.bfloat16)  17.7 us
  transfers between devices with their start and end apart: 3, of which 2 were waited for; matrix products, arithmetic and copies ran while one was open for 4% of the time, Pallas kernels for 0%

commit v1 on v0

v1 whole, which is shorter than its diff:
```python
import functools

import jax
import jax.numpy as jnp
from jax import lax
from jax.experimental import pallas as pl
from jax.experimental.pallas import tpu as pltpu
from jax.sharding import PartitionSpec as P

ROPE_DIM = 64
QK_DIM = 192
MESH = pl.DeviceIdType.MESH
NEG = -1e30

CACHE_SLOTS = 4
RING = 4
MERGE_LAG = 1
FINAL_LAG = 3


def _kernel(dims, len_ref, q_ref, cache_ref, out_ref, q_all, cbuf, o_tx, lse_acc, lse_tx, rx, rx_lse, m_tx, m_lse, rxm, rxm_lse,
            w_rows, o_stage, q_sem, c_sem, ag_send, ag_recv, o_send, o_recv, l_send, l_recv, m_send, m_recv, ml_send, ml_recv, out_sem):
    steps, group, heads, width, pages, page_len = dims
    latent = width - ROPE_DIM
    scale = QK_DIM ** -0.5
    me = lax.axis_index('dcp')
    core = me % 2
    x = (me // 2) % 2
    y = me // 4

    def dev(dx, dy, c):
        return ((y + dy) % 2 * 2 + (x + dx) % 2) * 2 + c

    n1x, n1y = core, 1 - core
    n2x, n2y = 1 - core, core
    n1 = dev(n1x, n1y, core)
    n2 = dev(n2x, n2y, core)
    partner = dev(0, 0, 1 - core)
    diag = dev(1, 1, core)

    owners = (
        dev(1, 1, 0), dev(1, 0, 0),
        dev(1, 1, 1), dev(0, 1, 1),
        dev(n2x, n2y, 1 - core), partner,
        dev(n1x, n1y, core), me,
    )
    targets = (dev(1, 0, 0), dev(0, 1, 1), partner)

    def to(device):
        return {'dcp': device}

    barrier = pltpu.get_barrier_semaphore()
    for other in range(1, group):
        pl.semaphore_signal(barrier, inc=1, device_id=to((me + other) % group), device_id_type=MESH)

    def q_load(u):
        return pltpu.make_async_copy(q_ref.at[:, u], q_all.at[u, :, me], q_sem.at[u])

    def c_load(i, r):
        slot = r % CACHE_SLOTS
        return pltpu.make_async_copy(cache_ref.at[owners[r] * steps + i, :, 0], cbuf.at[slot], c_sem.at[slot])

    def ag(u, kind):
        block = (me, me, me, n2, n2, n1, diag)[kind]
        target = (n2, n1, partner, n1, partner, partner, partner)[kind]
        return pltpu.make_async_remote_copy(
            src_ref=q_all.at[u, :, block], dst_ref=q_all.at[u, :, block],
            send_sem=ag_send.at[u, kind], recv_sem=ag_recv.at[u, kind],
            device_id=to(target), device_id_type=MESH)

    def ag_own(u):
        q_load(u).wait()
        for kind in range(3):
            ag(u, kind).start()

    def ag_forward(u):
        ag(u, 0).wait_recv()
        ag(u, 3).start()
        ag(u, 4).start()
        ag(u, 1).wait_recv()
        ag(u, 5).start()

    def ag_relay(u):
        ag(u, 3).wait_recv()
        ag(u, 6).start()

    def ag_ready(u):
        for kind in (2, 4, 5, 6):
            ag(u, kind).wait_recv()

    def o_copy(i, t):
        ring = i % RING
        dst = (0, 0, 2)[t]
        return pltpu.make_async_remote_copy(
            src_ref=o_tx.at[ring, t], dst_ref=rx.at[i, core if t < 2 else 2],
            send_sem=o_send.at[ring, t], recv_sem=o_recv.at[i, core if t < 2 else 2],
            device_id=to(targets[t]), device_id_type=MESH)

    def l_copy(i, t):
        ring = i % RING
        return pltpu.make_async_remote_copy(
            src_ref=lse_tx.at[ring], dst_ref=rx_lse.at[i, core if t < 2 else 2],
            send_sem=l_send.at[ring, t], recv_sem=l_recv.at[i, core if t < 2 else 2],
            device_id=to(targets[t]), device_id_type=MESH)

    def rx_wait(i, s):
        pltpu.make_async_remote_copy(
            src_ref=o_tx.at[0, 0], dst_ref=rx.at[i, s], send_sem=o_send.at[0, 0], recv_sem=o_recv.at[i, s],
            device_id=to(partner), device_id_type=MESH).wait_recv()
        pltpu.make_async_remote_copy(
            src_ref=lse_tx.at[0], dst_ref=rx_lse.at[i, s], send_sem=l_send.at[0, 0], recv_sem=l_recv.at[i, s],
            device_id=to(partner), device_id_type=MESH).wait_recv()

    def m_copy(i):
        ring = i % RING
        return pltpu.make_async_remote_copy(
            src_ref=m_tx.at[ring], dst_ref=rxm.at[i], send_sem=m_send.at[ring], recv_sem=m_recv.at[i],
            device_id=to(n1), device_id_type=MESH)

    def ml_copy(i):
        ring = i % RING
        return pltpu.make_async_remote_copy(
            src_ref=m_lse.at[ring], dst_ref=rxm_lse.at[i], send_sem=ml_send.at[ring], recv_sem=ml_recv.at[i],
            device_id=to(n1), device_id_type=MESH)

    def out_copy(i):
        return pltpu.make_async_copy(o_stage.at[i % 2], out_ref.at[i], out_sem.at[i % 2])

    lane = lax.broadcasted_iota(jnp.int32, (heads, 128), 1)
    col = lax.broadcasted_iota(jnp.int32, (1, page_len), 1)

    def attend(i, r):
        slot = r % CACHE_SLOTS
        c_load(i, r).wait()
        q = q_all[i, owners[r]].reshape(heads, width)
        length = len_ref[owners[r] * steps + i]
        scores = []
        for j in range(pages):
            s = lax.dot_general(q, cbuf[slot, j], (((1,), (0,)), ((), ())), preferred_element_type=jnp.float32) * scale
            first = (j * group + me) * page_len
            scores.append(jnp.where(col + first < length, s, NEG))
        row_max = functools.reduce(jnp.maximum, [jnp.max(s, axis=1, keepdims=True) for s in scores])
        total = jnp.zeros((heads, 1), jnp.float32)
        acc = jnp.zeros((heads, latent), jnp.float32)
        for j in range(pages):
            w = jnp.exp(scores[j] - row_max)
            total = total + jnp.sum(w, axis=1, keepdims=True)
            acc = acc + lax.dot_general(w.astype(jnp.bfloat16), cbuf[slot, j, :latent], (((1,), (1,)), ((), ())),
                                        preferred_element_type=jnp.float32)
        o_tx[i % RING, r // 2, r % 2] = (acc / total).astype(jnp.bfloat16)
        lse_acc[...] = jnp.where(lane == r, row_max + jnp.log(total), lse_acc[...])

    def weighted(rows, blocks):
        top = functools.reduce(jnp.maximum, rows)
        exps = [jnp.exp(v - top) for v in rows]
        total = functools.reduce(jnp.add, exps)
        lse = top + jnp.log(total)
        for n, v in enumerate(rows):
            w_rows[n:n + 1, :] = jnp.exp(v - lse)
        cols = w_rows[...].T
        acc = cols[:, 0:1] * blocks[0].astype(jnp.float32)
        for n in range(1, len(blocks)):
            acc = acc + cols[:, n:n + 1] * blocks[n].astype(jnp.float32)
        return lse, acc

    def pick(block, k):
        return jnp.where(core == 0, block[k:k + 1], block[2 + k:3 + k])

    def merge(i):
        ring = i % RING
        for s in range(3):
            rx_wait(i, s)
        rows = [lse_tx[ring][6:7], pick(rx_lse[i, 0], 0), pick(rx_lse[i, 1], 0), rx_lse[i, 2][4:5]]
        lse, acc = weighted(rows, [o_tx[ring, 3, 0], rx[i, 0, 0], rx[i, 1, 0], rx[i, 2, 0]])
        m_tx[ring] = acc
        m_lse[ring] = jnp.broadcast_to(lse, (8, heads))

    def final(i):
        ring = i % RING
        m_recv_wait(i)
        rows = [lse_tx[ring][7:8], pick(rx_lse[i, 0], 1), pick(rx_lse[i, 1], 1), rx_lse[i, 2][5:6], rxm_lse[i][0:1]]
        _, acc = weighted(rows, [o_tx[ring, 3, 1], rx[i, 0, 1], rx[i, 1, 1], rx[i, 2, 1], rxm[i]])
        o_stage[i % 2] = acc.astype(jnp.bfloat16)

    def m_recv_wait(i):
        m_copy(i).wait_recv()
        ml_copy(i).wait_recv()

    for r in range(CACHE_SLOTS - 1):
        c_load(0, r).start()

    @pl.loop(0, steps)
    def _(u):
        q_load(u).start()

    w_rows[...] = jnp.zeros_like(w_rows)
    lse_acc[...] = jnp.zeros_like(lse_acc)
    pl.semaphore_wait(barrier, group - 1)

    for u in range(4):
        ag_own(u)
    for u in range(2):
        ag_forward(u)
    for u in range(2):
        ag_relay(u)

    @pl.loop(0, steps + FINAL_LAG)
    def _(i):
        gathering = i < steps // 2 - 1

        @pl.when(i < steps)
        def _():
            @pl.when(i >= RING)
            def _():
                for t in range(3):
                    o_copy(i - RING, t).wait_send()
                    l_copy(i - RING, t).wait_send()

            ag_ready(i)
            for r in range(group):
                ahead = r + CACHE_SLOTS - 1
                if ahead < group:
                    c_load(i, ahead).start()
                else:
                    @pl.when(i + 1 < steps)
                    def _():
                        c_load(i + 1, ahead - group).start()
                attend(i, r)
                if r in (1, 3, 5):
                    o_copy(i, r // 2).start()
                if r in (0, 4):
                    @pl.when(i < steps // 2 - 2)
                    def _():
                        ag_own(2 * i + 4 + r // 4)
                if r in (2, 4):
                    @pl.when(gathering)
                    def _():
                        ag_forward(2 * i + 2 + r // 4)
                if r in (5, 7):
                    @pl.when(gathering)
                    def _():
                        ag_relay(2 * i + 2 + r // 6)
            lse_tx[i % RING] = lse_acc[...].T[0:8]
            for t in range(3):
                l_copy(i, t).start()

        @pl.when((i >= MERGE_LAG) & (i < steps + MERGE_LAG))
        def _():
            k = i - MERGE_LAG

            @pl.when(k >= RING)
            def _():
                m_copy(k - RING).wait_send()
                ml_copy(k - RING).wait_send()

            merge(k)
            m_copy(k).start()
            ml_copy(k).start()

        @pl.when(i >= FINAL_LAG)
        def _():
            k = i - FINAL_LAG

            @pl.when(k >= 2)
            def _():
                out_copy(k - 2).wait()

            final(k)
            out_copy(k).start()

    @pl.loop(steps - RING, steps)
    def _(i):
        for t in range(3):
            o_copy(i, t).wait_send()
            l_copy(i, t).wait_send()
        m_copy(i).wait_send()
        ml_copy(i).wait_send()

    @pl.loop(0, steps)
    def _(u):
        for kind in range(7):
            ag(u, kind).wait_send()

    for i in (steps - 2, steps - 1):
        out_copy(i).wait()


def solution(mesh):
    group = mesh.shape['dcp']

    def local_step(q_blk, cache_blk, len_blk):
        batch, own_heads, width = q_blk.shape
        pages, page_len = cache_blk.shape[1], cache_blk.shape[3]
        steps = batch // group
        heads = own_heads * group
        latent = width - ROPE_DIM
        bf16, f32 = jnp.bfloat16, jnp.float32
        dma = pltpu.SemaphoreType.DMA
        return pl.pallas_call(
            functools.partial(_kernel, (steps, group, heads, width, pages, page_len)),
            out_shape=jax.ShapeDtypeStruct((steps, heads, latent), bf16),
            in_specs=[pl.BlockSpec(memory_space=pltpu.SMEM), pl.BlockSpec(memory_space=pl.ANY), pl.BlockSpec(memory_space=pl.ANY)],
            out_specs=pl.BlockSpec(memory_space=pl.ANY),
            scratch_shapes=[
                pltpu.VMEM((steps, group, group, own_heads, width), bf16),
                pltpu.VMEM((CACHE_SLOTS, pages, width, page_len), bf16),
                pltpu.VMEM((RING, 4, 2, heads, latent), bf16),
                pltpu.VMEM((heads, 128), f32),
                pltpu.VMEM((RING, 8, heads), f32),
                pltpu.VMEM((steps, 3, 2, heads, latent), bf16),
                pltpu.VMEM((steps, 3, 8, heads), f32),
                pltpu.VMEM((RING, heads, latent), f32),
                pltpu.VMEM((RING, 8, heads), f32),
                pltpu.VMEM((steps, heads, latent), f32),
                pltpu.VMEM((steps, 8, heads), f32),
                pltpu.VMEM((128, heads), f32),
                pltpu.VMEM((2, heads, latent), bf16),
                dma((steps,)), dma((CACHE_SLOTS,)),
                dma((steps, 7)), dma((steps, 7)),
                dma((RING, 3)), dma((steps, 3)), dma((RING, 3)), dma((steps, 3)),
                dma((RING,)), dma((steps,)), dma((RING,)), dma((steps,)),
                dma((2,)),
            ],
            compiler_params=pltpu.CompilerParams(collective_id=0, has_side_effects=True, vmem_limit_bytes=66_000_000),
        )(len_blk, q_blk.reshape(group, steps, own_heads, width), jnp.swapaxes(cache_blk, 3, 4))

    return jax.shard_map(local_step, mesh=mesh, in_specs=(P('dp', 'dcp', None), P('dp', None, 'dcp', None, None), P('dp')),
                         out_specs=P(('dp', 'dcp'), None, None), check_vma=False)
```

time: 525 us -> 263 us (0.50)
  waiting for transfers between devices: 287 us -> 0 us
  Pallas kernels: 0 us -> 254 us
  matrix products: 162 us -> 0 us
  other arithmetic: 49.9 us -> 0 us
  between operations: 13.5 us -> 0.01 us
  starting transfers between devices: 6.58 us -> 0 us
    pallas_call x0 -> x1, Pallas kernels: none -> 254 us  [local_step(): pl.pallas_call(functools.partial(_kernel, (steps, group, heads, width, pa...]
    all_to_all x2 -> x0, waiting for transfers between devices: 184 us -> none  [the longest x1 184 us: local_step(): lax.all_to_all(part_out, 'dcp', 0, 0, tiled=True)]
    dot_general x2 -> x0, matrix products: 162 us -> none  [the longest x1 86.7 us: local_step(): jnp.einsum('bhjt,bjtw->bhw', weights_exp.astype(jnp.bfloat16), cache_own,...]
    all_gather x1 -> x0, waiting for transfers between devices: 104 us -> none  [local_step(): q_full = lax.all_gather(q_blk, 'dcp', axis=1, tiled=True)]
    reduce_sum x3 -> x0, other arithmetic: 30.5 us -> none  [the longest x1 21.5 us: local_step(): denom_sum = jnp.sum(weights_exp, axis=(2, 3))]
    convert_element_type x1 -> x0, other arithmetic: 17.7 us -> none  [local_step(): (pv_sum[..., :latent_dim] / denom_sum[..., None]).astype(jnp.bfloat16)]
    all_to_all x2 -> x0, starting transfers between devices: 6.58 us -> none  [the longest x1 4.49 us: local_step(): lax.all_to_all(part_out, 'dcp', 0, 0, tiled=True)]
  transfers between devices with their start and end apart: 3 -> 0, of which waited for: 2 -> 0; matrix products, arithmetic and copies ran while one was open for 4% -> 0% of each run, Pallas kernels for 0% -> 0%
where the time goes in v1:
time: 263 us; the launch traced here: 262 us
  Pallas kernels  254 us (97%)
  local copies, waits for them, and re-layouts  8.01 us (3%)
    pallas_call x1, Pallas kernels, local_step(): pl.pallas_call(functools.partial(_kernel, (steps, group, heads, width, pa...  254 us
    unnamed x2, local copies, waits for them, and re-layouts  8.01 us

profile of v1, /device:TPU:0, one launch (start us, length us, event | category | flops | bytes accessed | tf_op | source)
XLA Modules:
  0.0 262.4 jit_solution(7684638234362271796)
XLA Ops:
  0.0 4.9 %copy.4 = bf16[128,16,576]{2,1,0:T(8,128)(2,1)} copy(bf16[128,16,576]{0,2,1:T(8,128)(2,1)} %param.3) | data formatting | bytes 4718592 | tf_op args[0]
  4.9 254.4 %shard_map.37 = bf16[16,128,512]{2,1,0:T(8,128)(2,1)} custom-call(s32[128]{0:T(128)} %len_ref.1, bf16[8,16,16,576]{3,2,1,0:T(8,128)(2,1)} %bitcast.2, bf16[128,4,1,576,256]{4,3,2,1,0:T(8,128)(2,1)} %bitcast.1.cache_ref), custom_call_target="tpu_custom_call" | custom-call | tf_op jit(solution)/shard_map/pallas_call | solution.py:299
  259.3 3.1 %copy.6 = bf16[16,128,512]{2,1,0:T(8,128)(2,1)} copy(bf16[16,128,512]{2,1,0:T(8,128)(2,1)} %shard_map.37) | data formatting | bytes 4194304

commit v2 on v0

v2 whole, which is shorter than its diff:
```python
import functools

import jax
import jax.numpy as jnp
from jax import lax
from jax.experimental import pallas as pl
from jax.experimental.pallas import tpu as pltpu
from jax.sharding import PartitionSpec as P

ROPE_DIM = 64
QK_DIM = 192
MESH = pl.DeviceIdType.MESH
NEG = -1e30

CACHE_SLOTS = 4
RING = 4
LEAD = 1
FINAL_LAG = 1


def _kernel(dims, len_ref, q_ref, cache_ref, out_ref, q_all, cbuf, o_tx, lse_acc, lse_a, lse_b, rx_d, rx_f, rx_p, rx_la, rx_lb,
            m_tx, m_lse, rx_m, rx_ml, w_rows, o_stage, q_sem, c_sem, ag_send, ag_recv, d_send, d_recv, f_send, f_recv, p_send, p_recv,
            la_send, la_recv, lb_send, lb_recv, m_send, m_recv, ml_send, ml_recv, out_sem):
    steps, group, heads, latent, pages, page_len = dims
    scale = QK_DIM ** -0.5
    me = lax.axis_index('dcp')
    core = me % 2
    x = (me // 2) % 2
    y = me // 4

    def dev(dx, dy, c):
        return ((y + dy) % 2 * 2 + (x + dx) % 2) * 2 + c

    n1x, n1y = core, 1 - core
    n2x, n2y = 1 - core, core
    n1 = dev(n1x, n1y, core)
    n2 = dev(n2x, n2y, core)
    partner = dev(0, 0, 1 - core)
    diag = dev(1, 1, core)
    x0, y1 = dev(1, 0, 0), dev(0, 1, 1)

    OM, PM, D0, D1, F0, F1, PF, OF = range(8)
    owners = (
        dev(n1x, n1y, core),
        dev(n2x, n2y, 1 - core),
        dev(1, 1, 0), dev(1, 1, 1),
        x0, y1,
        partner, me,
    )

    def remote(src, dst, send, recv, device):
        return pltpu.make_async_remote_copy(src_ref=src, dst_ref=dst, send_sem=send, recv_sem=recv,
                                            device_id={'dcp': device}, device_id_type=MESH)

    barrier = pltpu.get_barrier_semaphore()
    for other in range(1, group):
        pl.semaphore_signal(barrier, inc=1, device_id={'dcp': (me + other) % group}, device_id_type=MESH)

    def q_load(u):
        return pltpu.make_async_copy(q_ref.at[u], q_all.at[u, :, me], q_sem.at[u])

    def row(it, p):
        return it if p in (D0, D1) else it - LEAD

    def valid(it, p):
        return it < steps if p in (D0, D1) else (it >= LEAD) & (it < steps + LEAD)

    def c_load(it, p):
        slot = p % CACHE_SLOTS
        return pltpu.make_async_copy(cache_ref.at[owners[p] * steps + row(it, p), :, 0], cbuf.at[slot], c_sem.at[slot])

    def out_copy(i):
        return pltpu.make_async_copy(o_stage.at[i % 2], out_ref.at[i], out_sem.at[i % 2])

    def ag(u, kind):
        block = (me, me, me, n2, n2, n1, diag)[kind]
        target = (n2, n1, partner, n1, partner, partner, partner)[kind]
        return remote(q_all.at[u, :, block], q_all.at[u, :, block], ag_send.at[u, kind], ag_recv.at[u, kind], target)

    def ag_own(u):
        q_load(u).wait()
        for kind in range(3):
            ag(u, kind).start()

    def ag_forward(u):
        ag(u, 0).wait_recv()
        ag(u, 3).start()
        ag(u, 4).start()
        ag(u, 1).wait_recv()
        ag(u, 5).start()

    def ag_relay(u):
        ag(u, 3).wait_recv()
        ag(u, 6).start()

    def ag_ready(u):
        for kind in (2, 4, 5, 6):
            ag(u, kind).wait_recv()

    def d_copy(it, t):
        ring = it % RING
        return remote(o_tx.at[ring, D0 + t], rx_d.at[it, core], d_send.at[ring, t], d_recv.at[it, core], (x0, y1)[t])

    def f_copy(it, t):
        ring, i = it % RING, it - LEAD
        return remote(o_tx.at[ring, F0 + t], rx_f.at[i, core], f_send.at[ring, t], f_recv.at[i, core], (x0, y1)[t])

    def p_copy(it, t):
        ring, i = it % RING, it - LEAD
        return remote(o_tx.at[ring, (PM, PF)[t]], rx_p.at[i, t], p_send.at[ring, t], p_recv.at[i, t], partner)

    def la_copy(it):
        ring, i = it % RING, it - LEAD
        return remote(lse_a.at[ring], rx_la.at[i], la_send.at[ring], la_recv.at[i], partner)

    def lb_copy(it, t):
        ring = it % RING
        s = core if t < 2 else 2
        return remote(lse_b.at[ring], rx_lb.at[it, s], lb_send.at[ring, t], lb_recv.at[it, s], (x0, y1, partner)[t])

    def m_copy(it):
        ring, i = it % RING, it - LEAD
        return remote(m_tx.at[ring], rx_m.at[i], m_send.at[ring], m_recv.at[i], n1)

    def ml_copy(it):
        ring, i = it % RING, it - LEAD
        return remote(m_lse.at[ring], rx_ml.at[i], ml_send.at[ring], ml_recv.at[i], n1)

    def sent(it):
        @pl.when(it < steps)
        def _():
            for t in range(2):
                d_copy(it, t).wait_send()

        @pl.when((it >= LEAD) & (it < steps + LEAD))
        def _():
            for t in range(2):
                f_copy(it, t).wait_send()
                p_copy(it, t).wait_send()
            la_copy(it).wait_send()
            m_copy(it).wait_send()
            ml_copy(it).wait_send()

        for t in range(3):
            lb_copy(it, t).wait_send()

    def landed(dst, recv, src):
        remote(src, dst, d_send.at[0, 0], recv, partner).wait_recv()

    lane = lax.broadcasted_iota(jnp.int32, (heads, 128), 1)
    col = lax.broadcasted_iota(jnp.int32, (1, page_len), 1)

    def attend(it, p, lse_row):
        slot = p % CACHE_SLOTS
        u, k = row(it, p), owners[p]
        c_load(it, p).wait()
        q = q_all[u, k].reshape(heads, latent)
        pair = q_all[u, group, :, :, pl.ds(pl.multiple_of(k // 2 * 128, 128), 128)].reshape(heads, 128)
        rope = jnp.where(k % 2 == 0, pair[:, :ROPE_DIM], pair[:, ROPE_DIM:])
        length = len_ref[k * steps + u]
        scores = []
        for j in range(pages):
            s = jnp.dot(q, cbuf[slot, j, :latent], preferred_element_type=jnp.float32)
            s = (s + jnp.dot(rope, cbuf[slot, j, latent:], preferred_element_type=jnp.float32)) * scale
            first = (j * group + me) * page_len
            scores.append(jnp.where(col + first < length, s, NEG))
        row_max = functools.reduce(jnp.maximum, [jnp.max(s, axis=1, keepdims=True) for s in scores])
        total = jnp.zeros((heads, 1), jnp.float32)
        acc = jnp.zeros((heads, latent), jnp.float32)
        for j in range(pages):
            w = jnp.exp(scores[j] - row_max)
            total = total + jnp.sum(w, axis=1, keepdims=True)
            acc = acc + lax.dot_general(w.astype(jnp.bfloat16), cbuf[slot, j, :latent], (((1,), (1,)), ((), ())),
                                        preferred_element_type=jnp.float32)
        o_tx[it % RING, p] = (acc / total).astype(jnp.bfloat16)
        lse_acc[...] = jnp.where(lane == lse_row, row_max + jnp.log(total), lse_acc[...])

    def weighted(rows, blocks):
        top = functools.reduce(jnp.maximum, rows)
        total = functools.reduce(jnp.add, [jnp.exp(v - top) for v in rows])
        lse = top + jnp.log(total)
        for n, v in enumerate(rows):
            w_rows[n:n + 1, :] = jnp.exp(v - lse)
        cols = w_rows[...].T
        acc = cols[:, 0:1] * blocks[0].astype(jnp.float32)
        for n in range(1, len(blocks)):
            acc = acc + cols[:, n:n + 1] * blocks[n].astype(jnp.float32)
        return lse, acc

    def pick(block, k):
        return jnp.where(core == 0, block[k:k + 1], block[k + 1:k + 2])

    def merge(it):
        ring, i = it % RING, it - LEAD
        for s in range(2):
            landed(rx_d.at[i, s], d_recv.at[i, s], o_tx.at[0, 0])
            landed(rx_lb.at[i, s], lb_recv.at[i, s], lse_b.at[0])
        p_copy(it, 0).wait_recv()
        la_copy(it).wait_recv()
        rows = [lse_a[ring][0:1], pick(rx_lb[i, 0], 0), pick(rx_lb[i, 1], 0), rx_la[i][1:2]]
        lse, acc = weighted(rows, [o_tx[ring, OM], rx_d[i, 0], rx_d[i, 1], rx_p[i, 0]])
        m_tx[ring] = acc
        m_lse[ring] = jnp.broadcast_to(lse, (8, heads))

    def final(it):
        ring, i = it % RING, it - LEAD
        for s in range(2):
            landed(rx_f.at[i, s], f_recv.at[i, s], o_tx.at[0, 0])

            @pl.when(it >= steps)
            def _():
                landed(rx_lb.at[it, s], lb_recv.at[it, s], lse_b.at[0])

        p_copy(it, 1).wait_recv()
        lb_copy(it, 2).wait_recv()
        m_copy(it).wait_recv()
        ml_copy(it).wait_recv()
        rows = [lse_b[ring][5:6], pick(rx_lb[it, 0], 2), pick(rx_lb[it, 1], 2), rx_lb[it, 2][4:5], rx_ml[i][0:1]]
        _, acc = weighted(rows, [o_tx[ring, OF], rx_f[i, 0], rx_f[i, 1], rx_p[i, 1], rx_m[i]])
        o_stage[i % 2] = acc.astype(jnp.bfloat16)

    @pl.loop(0, steps)
    def _(u):
        q_load(u).start()

    for p in range(CACHE_SLOTS - 1):
        if p in (D0, D1):
            c_load(0, p).start()

    w_rows[...] = jnp.zeros_like(w_rows)
    lse_acc[...] = jnp.zeros_like(lse_acc)
    pl.semaphore_wait(barrier, group - 1)

    ag_own(0)
    ag_own(1)
    ag_forward(0)
    ag_own(2)
    ag_forward(1)
    ag_relay(0)
    ag_own(3)
    ag_relay(1)

    def gather(it, phase):
        if phase == 0:
            @pl.when(it < steps // 2 - 2)
            def _():
                ag_own(2 * it + 4)
                ag_own(2 * it + 5)
        elif phase == 1:
            @pl.when(it < steps // 2 - 1)
            def _():
                ag_forward(2 * it + 2)
                ag_forward(2 * it + 3)
        else:
            @pl.when((it >= 1) & (it < steps // 2))
            def _():
                ag_relay(2 * it)
                ag_relay(2 * it + 1)

    @pl.loop(0, steps + LEAD + FINAL_LAG)
    def _(it):
        @pl.when(it >= RING)
        def _():
            sent(it - RING)

        @pl.when(it < steps)
        def _():
            ag_ready(it)

        gather(it, 0)
        for p in range(group):
            ahead = p + CACHE_SLOTS - 1
            nxt = it + ahead // group

            @pl.when(valid(nxt, ahead % group))
            def _():
                c_load(nxt, ahead % group).start()

            @pl.when(valid(it, p))
            def _():
                attend(it, p, (0, 1, 0, 1, 2, 3, 4, 5)[p])
                if p == PM:
                    lse_a[it % RING] = lse_acc[...].T[0:8]
                    p_copy(it, 0).start()
                    la_copy(it).start()
                elif p in (D0, D1):
                    d_copy(it, p - D0).start()
                elif p in (F0, F1):
                    f_copy(it, p - F0).start()
                elif p == PF:
                    p_copy(it, 1).start()
                if p == F1:
                    merge(it)
                    m_copy(it).start()
                    ml_copy(it).start()

            if p == D1:
                gather(it, 1)
            if p == F1:
                gather(it, 2)

        @pl.when(it < steps + LEAD)
        def _():
            lse_b[it % RING] = lse_acc[...].T[0:8]
            for t in range(3):
                lb_copy(it, t).start()

        @pl.when(it >= LEAD + FINAL_LAG)
        def _():
            k = it - FINAL_LAG

            @pl.when(k >= LEAD + 2)
            def _():
                out_copy(k - LEAD - 2).wait()

            final(k)
            out_copy(k - LEAD).start()

    @pl.loop(steps + LEAD + FINAL_LAG - RING, steps + LEAD)
    def _(it):
        sent(it)

    for it in range(LEAD):
        landed(rx_lb.at[it, 2], lb_recv.at[it, 2], lse_b.at[0])

    @pl.loop(0, steps)
    def _(u):
        for kind in range(7):
            ag(u, kind).wait_send()

    for i in (steps - 2, steps - 1):
        out_copy(i).wait()


def solution(mesh):
    group = mesh.shape['dcp']

    def local_step(q_blk, cache_blk, len_blk):
        batch, own_heads, width = q_blk.shape
        pages, page_len = cache_blk.shape[1], cache_blk.shape[3]
        steps = batch // group
        heads = own_heads * group
        latent = width - ROPE_DIM
        bf16, f32 = jnp.bfloat16, jnp.float32
        dma = pltpu.SemaphoreType.DMA
        q_steps = q_blk.reshape(group, steps, own_heads, width)
        q_latent = jnp.transpose(q_steps[..., :latent], (1, 0, 2, 3))
        q_rope = jnp.transpose(q_steps[..., latent:], (1, 2, 0, 3)).reshape(steps, 1, own_heads, group * ROPE_DIM)
        q_blocks = jnp.concatenate([q_latent, q_rope], axis=1)
        return pl.pallas_call(
            functools.partial(_kernel, (steps, group, heads, latent, pages, page_len)),
            out_shape=jax.ShapeDtypeStruct((steps, heads, latent), bf16),
            in_specs=[pl.BlockSpec(memory_space=pltpu.SMEM), pl.BlockSpec(memory_space=pl.ANY), pl.BlockSpec(memory_space=pl.ANY)],
            out_specs=pl.BlockSpec(memory_space=pl.ANY),
            scratch_shapes=[
                pltpu.VMEM((steps, group + 1, group, own_heads, latent), bf16),
                pltpu.VMEM((CACHE_SLOTS, pages, width, page_len), bf16),
                pltpu.VMEM((RING, group, heads, latent), bf16),
                pltpu.VMEM((heads, 128), f32),
                pltpu.VMEM((RING, 8, heads), f32),
                pltpu.VMEM((RING, 8, heads), f32),
                pltpu.VMEM((steps, 2, heads, latent), bf16),
                pltpu.VMEM((steps, 2, heads, latent), bf16),
                pltpu.VMEM((steps, 2, heads, latent), bf16),
                pltpu.VMEM((steps, 8, heads), f32),
                pltpu.VMEM((steps + LEAD, 3, 8, heads), f32),
                pltpu.VMEM((RING, heads, latent), f32),
                pltpu.VMEM((RING, 8, heads), f32),
                pltpu.VMEM((steps, heads, latent), f32),
                pltpu.VMEM((steps, 8, heads), f32),
                pltpu.VMEM((128, heads), f32),
                pltpu.VMEM((2, heads, latent), bf16),
                dma((steps,)), dma((CACHE_SLOTS,)),
                dma((steps, 7)), dma((steps, 7)),
                dma((RING, 2)), dma((steps, 2)),
                dma((RING, 2)), dma((steps, 2)),
                dma((RING, 2)), dma((steps, 2)),
                dma((RING,)), dma((steps,)),
                dma((RING, 3)), dma((steps + LEAD, 3)),
                dma((RING,)), dma((steps,)), dma((RING,)), dma((steps,)),
                dma((2,)),
            ],
            compiler_params=pltpu.CompilerParams(collective_id=0, has_side_effects=True, vmem_limit_bytes=66_000_000),
        )(len_blk, q_blocks, jnp.swapaxes(cache_blk, 3, 4))

    return jax.shard_map(local_step, mesh=mesh, in_specs=(P('dp', 'dcp', None), P('dp', None, 'dcp', None, None), P('dp')),
                         out_specs=P(('dp', 'dcp'), None, None), check_vma=False)
```

time: 525 us -> 236 us (0.45)
  waiting for transfers between devices: 287 us -> 0 us
  Pallas kernels: 0 us -> 226 us
  matrix products: 162 us -> 0 us
  other arithmetic: 49.9 us -> 1.64 us
  between operations: 13.5 us -> 0.05 us
  starting transfers between devices: 6.58 us -> 0 us
    pallas_call x0 -> x1, Pallas kernels: none -> 226 us  [local_step(): pl.pallas_call(functools.partial(_kernel, (steps, group, heads, latent, p...]
    all_to_all x2 -> x0, waiting for transfers between devices: 184 us -> none  [the longest x1 184 us: local_step(): lax.all_to_all(part_out, 'dcp', 0, 0, tiled=True)]
    dot_general x2 -> x0, matrix products: 162 us -> none  [the longest x1 86.7 us: local_step(): jnp.einsum('bhjt,bjtw->bhw', weights_exp.astype(jnp.bfloat16), cache_own,...]
    all_gather x1 -> x0, waiting for transfers between devices: 104 us -> none  [local_step(): q_full = lax.all_gather(q_blk, 'dcp', axis=1, tiled=True)]
    reduce_sum x3 -> x0, other arithmetic: 30.5 us -> none  [the longest x1 21.5 us: local_step(): denom_sum = jnp.sum(weights_exp, axis=(2, 3))]
    convert_element_type x1 -> x0, other arithmetic: 17.7 us -> none  [local_step(): (pv_sum[..., :latent_dim] / denom_sum[..., None]).astype(jnp.bfloat16)]
    all_to_all x2 -> x0, starting transfers between devices: 6.58 us -> none  [the longest x1 4.49 us: local_step(): lax.all_to_all(part_out, 'dcp', 0, 0, tiled=True)]
  transfers between devices with their start and end apart: 3 -> 0, of which waited for: 2 -> 0; matrix products, arithmetic and copies ran while one was open for 4% -> 0% of each run, Pallas kernels for 0% -> 0%
where the time goes in v2:
time: 236 us
  Pallas kernels  226 us (96%)
  local copies, waits for them, and re-layouts  8.04 us (3%)
    pallas_call x1, Pallas kernels, local_step(): pl.pallas_call(functools.partial(_kernel, (steps, group, heads, latent, p...  226 us
    unnamed x2, local copies, waits for them, and re-layouts  7 us

profile of v2, /device:TPU:0, one launch (start us, length us, event | category | flops | bytes accessed | tf_op | source)
XLA Modules:
  0.0 235.8 jit_solution(5740672181268097320)
XLA Ops:
  0.0 3.9 %copy.5 = bf16[128,16,576]{2,1,0:T(8,128)(2,1)S(1)} copy(bf16[128,16,576]{0,2,1:T(8,128)(2,1)} %param.3) | data formatting | bytes 4718592 | tf_op args[0]
  3.9 0.1 slice_bitcast_fusion
  4.0 0.3 copy.7
  4.4 0.3 reshape.7
  4.7 0.3 copy_bitcast_fusion
  5.0 1.6 pad_maximum_fusion.q_ref
  6.6 226.1 %shard_map.37 = bf16[16,128,512]{2,1,0:T(8,128)(2,1)} custom-call(s32[128]{0:T(128)} %len_ref.1, bf16[16,9,16,512]{3,2,1,0:T(8,128)(2,1)} %pad_maximum_fusion.q_ref, bf16[128,4,1,576,256]{4,3,2,1,0:T(8,128)(2,1)} %bitcast.3.cache_ref), custom_call_target="tpu_custom_call" | custom-call | tf_op jit(solution)/shard_map/pallas_call | solution.py:350
  232.7 3.1 %copy.11 = bf16[16,128,512]{2,1,0:T(8,128)(2,1)} copy(bf16[16,128,512]{2,1,0:T(8,128)(2,1)} %shard_map.37) | data formatting | bytes 4194304

commit v3 on v2

--- a/solution.py
+++ b/solution.py
@@ -18,8 +18,8 @@
 FINAL_LAG = 1
 
 
-def _kernel(dims, len_ref, q_ref, cache_ref, out_ref, q_all, cbuf, o_tx, lse_acc, lse_a, lse_b, rx_d, rx_f, rx_p, rx_la, rx_lb,
-            m_tx, m_lse, rx_m, rx_ml, w_rows, o_stage, q_sem, c_sem, ag_send, ag_recv, d_send, d_recv, f_send, f_recv, p_send, p_recv,
+def _kernel(dims, len_hbm, q_hbm, cache_ref, out_ref, len_ref, q_own, q_all, cbuf, o_tx, lse_acc, lse_a, lse_b, rx_d, rx_f, rx_p, rx_la, rx_lb,
+            m_tx, m_lse, rx_m, rx_ml, w_rows, o_stage, len_sem, q_sem, c_sem, ag_send, ag_recv, d_send, d_recv, f_send, f_recv, p_send, p_recv,
             la_send, la_recv, lb_send, lb_recv, m_send, m_recv, ml_send, ml_recv, out_sem):
     steps, group, heads, latent, pages, page_len = dims
     scale = QK_DIM ** -0.5
@@ -56,8 +56,11 @@
     for other in range(1, group):
         pl.semaphore_signal(barrier, inc=1, device_id={'dcp': (me + other) % group}, device_id_type=MESH)
 
-    def q_load(u):
-        return pltpu.make_async_copy(q_ref.at[u], q_all.at[u, :, me], q_sem.at[u])
+    def len_load():
+        return pltpu.make_async_copy(len_hbm, len_ref, len_sem)
+
+    def q_load():
+        return pltpu.make_async_copy(q_hbm, q_own, q_sem)
 
     def row(it, p):
         return it if p in (D0, D1) else it - LEAD
@@ -77,8 +80,25 @@
         target = (n2, n1, partner, n1, partner, partner, partner)[kind]
         return remote(q_all.at[u, :, block], q_all.at[u, :, block], ag_send.at[u, kind], ag_recv.at[u, kind], target)
 
+    wide_row = lax.broadcasted_iota(jnp.int32, (heads, steps * group), 0)
+    wide_lane = lax.broadcasted_iota(jnp.int32, (heads, steps * group), 1)
+    own_heads = heads // group
+    own_head = wide_row % own_heads
+
+    def q_build(u):
+        chosen = wide_lane == wide_row // own_heads * steps + u
+        acc = None
+        for h in range(0, own_heads, 2):
+            one_hot = jnp.concatenate([jnp.where(chosen & (own_head == g), 1.0, 0.0) for g in (h, h + 1)], axis=1)
+            pair = jnp.concatenate([q_own[h], q_own[h + 1]], axis=1)
+            term = lax.dot_general(one_hot.astype(jnp.bfloat16), pair, (((1,), (1,)), ((), ())), preferred_element_type=jnp.float32)
+            acc = term if acc is None else acc + term
+        q_all[u, 0:group, me] = acc[:, :latent].astype(jnp.bfloat16).reshape(group, own_heads, latent)
+        ropes = [acc[k * own_heads:(k + 1) * own_heads, latent:] for k in range(group)]
+        q_all[u, group, me] = jnp.concatenate(ropes, axis=1).astype(jnp.bfloat16)
+
     def ag_own(u):
-        q_load(u).wait()
+        q_build(u)
         for kind in range(3):
             ag(u, kind).start()
 
@@ -116,7 +136,7 @@
     def lb_copy(it, t):
         ring = it % RING
         s = core if t < 2 else 2
-        return remote(lse_b.at[ring], rx_lb.at[it, s], lb_send.at[ring, t], lb_recv.at[it, s], (x0, y1, partner)[t])
+        return remote(lse_b.at[ring, t], rx_lb.at[it, s], lb_send.at[ring, t], lb_recv.at[it, s], (x0, y1, partner)[t])
 
     def m_copy(it):
         ring, i = it % RING, it - LEAD
@@ -187,20 +207,17 @@
             acc = acc + cols[:, n:n + 1] * blocks[n].astype(jnp.float32)
         return lse, acc
 
-    def pick(block, k):
-        return jnp.where(core == 0, block[k:k + 1], block[k + 1:k + 2])
-
     def merge(it):
         ring, i = it % RING, it - LEAD
         for s in range(2):
             landed(rx_d.at[i, s], d_recv.at[i, s], o_tx.at[0, 0])
-            landed(rx_lb.at[i, s], lb_recv.at[i, s], lse_b.at[0])
+            landed(rx_lb.at[i, s], lb_recv.at[i, s], lse_b.at[0, 0])
         p_copy(it, 0).wait_recv()
         la_copy(it).wait_recv()
-        rows = [lse_a[ring][0:1], pick(rx_lb[i, 0], 0), pick(rx_lb[i, 1], 0), rx_la[i][1:2]]
+        rows = [lse_a[ring][0:1], rx_lb[i, 0][0:1], rx_lb[i, 1][0:1], rx_la[i][1:2]]
         lse, acc = weighted(rows, [o_tx[ring, OM], rx_d[i, 0], rx_d[i, 1], rx_p[i, 0]])
         m_tx[ring] = acc
-        m_lse[ring] = jnp.broadcast_to(lse, (8, heads))
+        m_lse[ring] = lse
 
     def final(it):
         ring, i = it % RING, it - LEAD
@@ -209,26 +226,25 @@
 
             @pl.when(it >= steps)
             def _():
-                landed(rx_lb.at[it, s], lb_recv.at[it, s], lse_b.at[0])
+                landed(rx_lb.at[it, s], lb_recv.at[it, s], lse_b.at[0, 0])
 
         p_copy(it, 1).wait_recv()
         lb_copy(it, 2).wait_recv()
         m_copy(it).wait_recv()
         ml_copy(it).wait_recv()
-        rows = [lse_b[ring][5:6], pick(rx_lb[it, 0], 2), pick(rx_lb[it, 1], 2), rx_lb[it, 2][4:5], rx_ml[i][0:1]]
+        rows = [lse_b[ring, 2][1:2], rx_lb[it, 0][1:2], rx_lb[it, 1][1:2], rx_lb[it, 2][0:1], rx_ml[i]]
         _, acc = weighted(rows, [o_tx[ring, OF], rx_f[i, 0], rx_f[i, 1], rx_p[i, 1], rx_m[i]])
         o_stage[i % 2] = acc.astype(jnp.bfloat16)
 
-    @pl.loop(0, steps)
-    def _(u):
-        q_load(u).start()
-
+    q_load().start()
+    len_load().start()
     for p in range(CACHE_SLOTS - 1):
         if p in (D0, D1):
             c_load(0, p).start()
 
     w_rows[...] = jnp.zeros_like(w_rows)
     lse_acc[...] = jnp.zeros_like(lse_acc)
+    q_load().wait()
     pl.semaphore_wait(barrier, group - 1)
 
     ag_own(0)
@@ -239,6 +255,7 @@
     ag_relay(0)
     ag_own(3)
     ag_relay(1)
+    len_load().wait()
 
     def gather(it, phase):
         if phase == 0:
@@ -278,9 +295,9 @@
 
             @pl.when(valid(it, p))
             def _():
-                attend(it, p, (0, 1, 0, 1, 2, 3, 4, 5)[p])
+                attend(it, p, (6, 7, 0, 2, 1, 3, 4, 5)[p])
                 if p == PM:
-                    lse_a[it % RING] = lse_acc[...].T[0:8]
+                    lse_a[it % RING] = lse_acc[...].T[6:8]
                     p_copy(it, 0).start()
                     la_copy(it).start()
                 elif p in (D0, D1):
@@ -301,7 +318,9 @@
 
         @pl.when(it < steps + LEAD)
         def _():
-            lse_b[it % RING] = lse_acc[...].T[0:8]
+            rows = lse_acc[...].T
+            for t in range(3):
+                lse_b[it % RING, t] = rows[2 * t:2 * t + 2]
             for t in range(3):
                 lb_copy(it, t).start()
 
@@ -321,7 +340,7 @@
         sent(it)
 
     for it in range(LEAD):
-        landed(rx_lb.at[it, 2], lb_recv.at[it, 2], lse_b.at[0])
+        landed(rx_lb.at[it, 2], lb_recv.at[it, 2], lse_b.at[0, 0])
 
     @pl.loop(0, steps)
     def _(u):
@@ -343,34 +362,32 @@
         latent = width - ROPE_DIM
         bf16, f32 = jnp.bfloat16, jnp.float32
         dma = pltpu.SemaphoreType.DMA
-        q_steps = q_blk.reshape(group, steps, own_heads, width)
-        q_latent = jnp.transpose(q_steps[..., :latent], (1, 0, 2, 3))
-        q_rope = jnp.transpose(q_steps[..., latent:], (1, 2, 0, 3)).reshape(steps, 1, own_heads, group * ROPE_DIM)
-        q_blocks = jnp.concatenate([q_latent, q_rope], axis=1)
         return pl.pallas_call(
             functools.partial(_kernel, (steps, group, heads, latent, pages, page_len)),
             out_shape=jax.ShapeDtypeStruct((steps, heads, latent), bf16),
-            in_specs=[pl.BlockSpec(memory_space=pltpu.SMEM), pl.BlockSpec(memory_space=pl.ANY), pl.BlockSpec(memory_space=pl.ANY)],
+            in_specs=[pl.BlockSpec(memory_space=pl.ANY)] * 3,
             out_specs=pl.BlockSpec(memory_space=pl.ANY),
             scratch_shapes=[
+                pltpu.SMEM((batch,), jnp.int32),
+                pltpu.VMEM((own_heads, width, batch), bf16),
                 pltpu.VMEM((steps, group + 1, group, own_heads, latent), bf16),
                 pltpu.VMEM((CACHE_SLOTS, pages, width, page_len), bf16),
                 pltpu.VMEM((RING, group, heads, latent), bf16),
                 pltpu.VMEM((heads, 128), f32),
-                pltpu.VMEM((RING, 8, heads), f32),
-                pltpu.VMEM((RING, 8, heads), f32),
+                pltpu.VMEM((RING, 2, heads), f32),
+                pltpu.VMEM((RING, 3, 2, heads), f32),
                 pltpu.VMEM((steps, 2, heads, latent), bf16),
                 pltpu.VMEM((steps, 2, heads, latent), bf16),
                 pltpu.VMEM((steps, 2, heads, latent), bf16),
-                pltpu.VMEM((steps, 8, heads), f32),
-                pltpu.VMEM((steps + LEAD, 3, 8, heads), f32),
+                pltpu.VMEM((steps, 2, heads), f32),
+                pltpu.VMEM((steps + LEAD, 3, 2, heads), f32),
                 pltpu.VMEM((RING, heads, latent), f32),
-                pltpu.VMEM((RING, 8, heads), f32),
+                pltpu.VMEM((RING, 1, heads), f32),
                 pltpu.VMEM((steps, heads, latent), f32),
-                pltpu.VMEM((steps, 8, heads), f32),
+                pltpu.VMEM((steps, 1, heads), f32),
                 pltpu.VMEM((128, heads), f32),
                 pltpu.VMEM((2, heads, latent), bf16),
-                dma((steps,)), dma((CACHE_SLOTS,)),
+                dma, dma, dma((CACHE_SLOTS,)),
                 dma((steps, 7)), dma((steps, 7)),
                 dma((RING, 2)), dma((steps, 2)),
                 dma((RING, 2)), dma((steps, 2)),
@@ -381,7 +398,7 @@
                 dma((2,)),
             ],
             compiler_params=pltpu.CompilerParams(collective_id=0, has_side_effects=True, vmem_limit_bytes=66_000_000),
-        )(len_blk, q_blocks, jnp.swapaxes(cache_blk, 3, 4))
+        )(len_blk, jnp.transpose(q_blk, (1, 2, 0)), jnp.swapaxes(cache_blk, 3, 4))
 
     return jax.shard_map(local_step, mesh=mesh, in_specs=(P('dp', 'dcp', None), P('dp', None, 'dcp', None, None), P('dp')),
                          out_specs=P(('dp', 'dcp'), None, None), check_vma=False)

time: 236 us -> 229 us (0.970)
  local copies, waits for them, and re-layouts: 8.04 us -> 3.1 us
    unnamed x2 -> x1, local copies, waits for them, and re-layouts: 7 us -> 3.1 us
where the time goes in v3:
time: 229 us
  Pallas kernels  226 us (99%)
  local copies, waits for them, and re-layouts  3.1 us (1%)
    pallas_call x1, Pallas kernels, local_step(): pl.pallas_call(functools.partial(_kernel, (steps, group, heads, latent, p...  226 us

profile of v3, /device:TPU:0, one launch (start us, length us, event | category | flops | bytes accessed | tf_op | source)
XLA Modules:
  0.0 228.8 jit_solution(10129416686512689764)
XLA Ops:
  0.0 225.7 %shard_map.37 = bf16[16,128,512]{2,1,0:T(8,128)(2,1)} custom-call(s32[128]{0:T(128)} %len_hbm.1, bf16[16,576,128]{2,1,0:T(8,128)(2,1)} %bitcast.2, bf16[128,4,1,576,256]{4,3,2,1,0:T(8,128)(2,1)} %bitcast.1.cache_ref), custom_call_target="tpu_custom_call" | custom-call | tf_op jit(solution)/shard_map/pallas_call | solution.py:365
  225.7 3.1 %copy.5 = bf16[16,128,512]{2,1,0:T(8,128)(2,1)} copy(bf16[16,128,512]{2,1,0:T(8,128)(2,1)} %shard_map.37) | data formatting | bytes 4194304

commit v4 on v3

--- a/solution.py
+++ b/solution.py
@@ -14,13 +14,14 @@
 
 CACHE_SLOTS = 4
 RING = 4
+AG_RING = 8
 LEAD = 1
 FINAL_LAG = 1
 
 
-def _kernel(dims, len_hbm, q_hbm, cache_ref, out_ref, len_ref, q_own, q_all, cbuf, o_tx, lse_acc, lse_a, lse_b, rx_d, rx_f, rx_p, rx_la, rx_lb,
-            m_tx, m_lse, rx_m, rx_ml, w_rows, o_stage, len_sem, q_sem, c_sem, ag_send, ag_recv, d_send, d_recv, f_send, f_recv, p_send, p_recv,
-            la_send, la_recv, lb_send, lb_recv, m_send, m_recv, ml_send, ml_recv, out_sem):
+def _kernel(dims, len_hbm, q_hbm, cache_ref, out_ref, len_ref, q_own, q_all, cbuf, o_tx, lse_acc, lse_a, lse_b, rx_d, rx_f, rx_la, rx_lb,
+            m_tx, m_lse, rx_m, rx_ml, w_rows, o_stage, len_sem, q_sem, c_sem, out_sem, ag_send, ag_recv, ag_part,
+            d_send, f_send, la_send, lb_send, m_send, ml_send, d_recv, f_recv, la_recv, lb_recv, m_recv, ml_recv):
     steps, group, heads, latent, pages, page_len = dims
     scale = QK_DIM ** -0.5
     me = lax.axis_index('dcp')
@@ -53,8 +54,9 @@
                                             device_id={'dcp': device}, device_id_type=MESH)
 
     barrier = pltpu.get_barrier_semaphore()
-    for other in range(1, group):
-        pl.semaphore_signal(barrier, inc=1, device_id={'dcp': (me + other) % group}, device_id_type=MESH)
+    peers = (n1, n2, partner)
+    for peer in peers:
+        pl.semaphore_signal(barrier, inc=1, device_id={'dcp': peer}, device_id_type=MESH)
 
     def len_load():
         return pltpu.make_async_copy(len_hbm, len_ref, len_sem)
@@ -78,7 +80,8 @@
     def ag(u, kind):
         block = (me, me, me, n2, n2, n1, diag)[kind]
         target = (n2, n1, partner, n1, partner, partner, partner)[kind]
-        return remote(q_all.at[u, :, block], q_all.at[u, :, block], ag_send.at[u, kind], ag_recv.at[u, kind], target)
+        recv = ag_part.at[u] if kind in (2, 4, 5, 6) else ag_recv.at[u % AG_RING, (0, 1, None, 2)[kind]]
+        return remote(q_all.at[u, :, block], q_all.at[u, :, block], ag_send.at[kind], recv, target)
 
     wide_row = lax.broadcasted_iota(jnp.int32, (heads, steps * group), 0)
     wide_lane = lax.broadcasted_iota(jnp.int32, (heads, steps * group), 1)
@@ -99,6 +102,9 @@
 
     def ag_own(u):
         q_build(u)
+        ag_send_own(u)
+
+    def ag_send_own(u):
         for kind in range(3):
             ag(u, kind).start()
 
@@ -114,58 +120,55 @@
         ag(u, 6).start()
 
     def ag_ready(u):
-        for kind in (2, 4, 5, 6):
-            ag(u, kind).wait_recv()
+        pltpu.make_async_copy(q_all.at[u, :, 0:4], q_all.at[u, :, 0:4], ag_part.at[u]).wait()
 
     def d_copy(it, t):
         ring = it % RING
-        return remote(o_tx.at[ring, D0 + t], rx_d.at[it, core], d_send.at[ring, t], d_recv.at[it, core], (x0, y1)[t])
+        return remote(o_tx.at[ring, D0 + t], rx_d.at[it, core], d_send.at[ring], d_recv.at[ring], (x0, y1)[t])
+
+    def pm_copy(it):
+        ring, i = it % RING, it - LEAD
+        return remote(o_tx.at[ring, PM], rx_d.at[i, 2], f_send.at[ring], d_recv.at[i % RING], partner)
 
     def f_copy(it, t):
         ring, i = it % RING, it - LEAD
-        return remote(o_tx.at[ring, F0 + t], rx_f.at[i, core], f_send.at[ring, t], f_recv.at[i, core], (x0, y1)[t])
-
-    def p_copy(it, t):
-        ring, i = it % RING, it - LEAD
-        return remote(o_tx.at[ring, (PM, PF)[t]], rx_p.at[i, t], p_send.at[ring, t], p_recv.at[i, t], partner)
+        return remote(o_tx.at[ring, (F0, F1, PF)[t]], rx_f.at[i, core if t < 2 else 2], f_send.at[ring], f_recv.at[ring],
+                      (x0, y1, partner)[t])
 
     def la_copy(it):
         ring, i = it % RING, it - LEAD
-        return remote(lse_a.at[ring], rx_la.at[i], la_send.at[ring], la_recv.at[i], partner)
+        return remote(lse_a.at[ring], rx_la.at[i], la_send.at[ring], la_recv.at[ring], partner)
 
     def lb_copy(it, t):
         ring = it % RING
-        s = core if t < 2 else 2
-        return remote(lse_b.at[ring, t], rx_lb.at[it, s], lb_send.at[ring, t], lb_recv.at[it, s], (x0, y1, partner)[t])
+        return remote(lse_b.at[ring, t], rx_lb.at[it, core if t < 2 else 2], lb_send.at[ring], lb_recv.at[ring], (x0, y1, partner)[t])
 
     def m_copy(it):
         ring, i = it % RING, it - LEAD
-        return remote(m_tx.at[ring], rx_m.at[i], m_send.at[ring], m_recv.at[i], n1)
+        return remote(m_tx.at[ring], rx_m.at[i], m_send.at[ring], m_recv.at[ring], n1)
 
     def ml_copy(it):
         ring, i = it % RING, it - LEAD
-        return remote(m_lse.at[ring], rx_ml.at[i], ml_send.at[ring], ml_recv.at[i], n1)
+        return remote(m_lse.at[ring], rx_ml.at[i], ml_send.at[ring], ml_recv.at[ring], n1)
+
+    def wait_bytes(ref, sem):
+        pltpu.make_async_copy(ref, ref, sem).wait()
 
     def sent(it):
+        ring = it % RING
+
         @pl.when(it < steps)
         def _():
-            for t in range(2):
-                d_copy(it, t).wait_send()
+            wait_bytes(o_tx.at[ring, 0:2], d_send.at[ring])
 
         @pl.when((it >= LEAD) & (it < steps + LEAD))
         def _():
-            for t in range(2):
-                f_copy(it, t).wait_send()
-                p_copy(it, t).wait_send()
-            la_copy(it).wait_send()
-            m_copy(it).wait_send()
-            ml_copy(it).wait_send()
-
-        for t in range(3):
-            lb_copy(it, t).wait_send()
-
-    def landed(dst, recv, src):
-        remote(src, dst, d_send.at[0, 0], recv, partner).wait_recv()
+            wait_bytes(o_tx.at[ring, 0:4], f_send.at[ring])
+            wait_bytes(lse_a.at[ring], la_send.at[ring])
+            wait_bytes(m_tx.at[ring], m_send.at[ring])
+            wait_bytes(m_lse.at[ring], ml_send.at[ring])
+
+        wait_bytes(lse_b.at[ring], lb_send.at[ring])
 
     lane = lax.broadcasted_iota(jnp.int32, (heads, 128), 1)
     col = lax.broadcasted_iota(jnp.int32, (1, page_len), 1)
@@ -209,31 +212,26 @@
 
     def merge(it):
         ring, i = it % RING, it - LEAD
-        for s in range(2):
-            landed(rx_d.at[i, s], d_recv.at[i, s], o_tx.at[0, 0])
-            landed(rx_lb.at[i, s], lb_recv.at[i, s], lse_b.at[0, 0])
-        p_copy(it, 0).wait_recv()
-        la_copy(it).wait_recv()
+        wait_bytes(rx_d.at[i], d_recv.at[i % RING])
+        wait_bytes(rx_lb.at[i], lb_recv.at[i % RING])
+        wait_bytes(rx_la.at[i], la_recv.at[ring])
         rows = [lse_a[ring][0:1], rx_lb[i, 0][0:1], rx_lb[i, 1][0:1], rx_la[i][1:2]]
-        lse, acc = weighted(rows, [o_tx[ring, OM], rx_d[i, 0], rx_d[i, 1], rx_p[i, 0]])
+        lse, acc = weighted(rows, [o_tx[ring, OM], rx_d[i, 0], rx_d[i, 1], rx_d[i, 2]])
         m_tx[ring] = acc
         m_lse[ring] = lse
 
     def final(it):
         ring, i = it % RING, it - LEAD
-        for s in range(2):
-            landed(rx_f.at[i, s], f_recv.at[i, s], o_tx.at[0, 0])
-
-            @pl.when(it >= steps)
-            def _():
-                landed(rx_lb.at[it, s], lb_recv.at[it, s], lse_b.at[0, 0])
-
-        p_copy(it, 1).wait_recv()
-        lb_copy(it, 2).wait_recv()
-        m_copy(it).wait_recv()
-        ml_copy(it).wait_recv()
+        wait_bytes(rx_f.at[i], f_recv.at[ring])
+
+        @pl.when(it >= steps)
+        def _():
+            wait_bytes(rx_lb.at[it], lb_recv.at[ring])
+
+        wait_bytes(rx_m.at[i], m_recv.at[ring])
+        wait_bytes(rx_ml.at[i], ml_recv.at[ring])
         rows = [lse_b[ring, 2][1:2], rx_lb[it, 0][1:2], rx_lb[it, 1][1:2], rx_lb[it, 2][0:1], rx_ml[i]]
-        _, acc = weighted(rows, [o_tx[ring, OF], rx_f[i, 0], rx_f[i, 1], rx_p[i, 1], rx_m[i]])
+        _, acc = weighted(rows, [o_tx[ring, OF], rx_f[i, 0], rx_f[i, 1], rx_f[i, 2], rx_m[i]])
         o_stage[i % 2] = acc.astype(jnp.bfloat16)
 
     q_load().start()
@@ -245,9 +243,10 @@
     w_rows[...] = jnp.zeros_like(w_rows)
     lse_acc[...] = jnp.zeros_like(lse_acc)
     q_load().wait()
-    pl.semaphore_wait(barrier, group - 1)
-
-    ag_own(0)
+    q_build(0)
+    pl.semaphore_wait(barrier, len(peers))
+
+    ag_send_own(0)
     ag_own(1)
     ag_forward(0)
     ag_own(2)
@@ -298,14 +297,14 @@
                 attend(it, p, (6, 7, 0, 2, 1, 3, 4, 5)[p])
                 if p == PM:
                     lse_a[it % RING] = lse_acc[...].T[6:8]
-                    p_copy(it, 0).start()
+                    pm_copy(it).start()
                     la_copy(it).start()
                 elif p in (D0, D1):
                     d_copy(it, p - D0).start()
                 elif p in (F0, F1):
                     f_copy(it, p - F0).start()
                 elif p == PF:
-                    p_copy(it, 1).start()
+                    f_copy(it, 2).start()
                 if p == F1:
                     merge(it)
                     m_copy(it).start()
@@ -339,13 +338,8 @@
     def _(it):
         sent(it)
 
-    for it in range(LEAD):
-        landed(rx_lb.at[it, 2], lb_recv.at[it, 2], lse_b.at[0, 0])
-
-    @pl.loop(0, steps)
-    def _(u):
-        for kind in range(7):
-            ag(u, kind).wait_send()
+    for kind in range(7):
+        wait_bytes(q_all.at[:, :, kind], ag_send.at[kind])
 
     for i in (steps - 2, steps - 1):
         out_copy(i).wait()
@@ -376,9 +370,8 @@
                 pltpu.VMEM((heads, 128), f32),
                 pltpu.VMEM((RING, 2, heads), f32),
                 pltpu.VMEM((RING, 3, 2, heads), f32),
-                pltpu.VMEM((steps, 2, heads, latent), bf16),
-                pltpu.VMEM((steps, 2, heads, latent), bf16),
-                pltpu.VMEM((steps, 2, heads, latent), bf16),
+                pltpu.VMEM((steps, 3, heads, latent), bf16),
+                pltpu.VMEM((steps, 3, heads, latent), bf16),
                 pltpu.VMEM((steps, 2, heads), f32),
                 pltpu.VMEM((steps + LEAD, 3, 2, heads), f32),
                 pltpu.VMEM((RING, heads, latent), f32),
@@ -387,15 +380,9 @@
                 pltpu.VMEM((steps, 1, heads), f32),
                 pltpu.VMEM((128, heads), f32),
                 pltpu.VMEM((2, heads, latent), bf16),
-                dma, dma, dma((CACHE_SLOTS,)),
-                dma((steps, 7)), dma((steps, 7)),
-                dma((RING, 2)), dma((steps, 2)),
-                dma((RING, 2)), dma((steps, 2)),
-                dma((RING, 2)), dma((steps, 2)),
-                dma((RING,)), dma((steps,)),
-                dma((RING, 3)), dma((steps + LEAD, 3)),
-                dma((RING,)), dma((steps,)), dma((RING,)), dma((steps,)),
-                dma((2,)),
+                dma, dma, dma((CACHE_SLOTS,)), dma((2,)),
+                dma((7,)), dma((AG_RING, 3)), dma((steps,)),
+                *[dma((RING,))] * 12,
             ],
             compiler_params=pltpu.CompilerParams(collective_id=0, has_side_effects=True, vmem_limit_bytes=66_000_000),
         )(len_blk, jnp.transpose(q_blk, (1, 2, 0)), jnp.swapaxes(cache_blk, 3, 4))

time: 229 us -> 226 us (0.987)
  Pallas kernels: 226 us -> 222 us
    pallas_call x1, Pallas kernels: 226 us -> 222 us  [local_step(): pl.pallas_call(functools.partial(_kernel, (steps, group, heads, latent, p...]
where the time goes in v4:
time: 226 us; the launch traced here: 225 us
  Pallas kernels  222 us (98%)
  local copies, waits for them, and re-layouts  3.1 us (1%)
    pallas_call x1, Pallas kernels, local_step(): pl.pallas_call(functools.partial(_kernel, (steps, group, heads, latent, p...  222 us

profile of v4, /device:TPU:0, one launch (start us, length us, event | category | flops | bytes accessed | tf_op | source)
XLA Modules:
  0.0 225.4 jit_solution(6360470759867437688)
XLA Ops:
  0.0 222.3 %shard_map.37 = bf16[16,128,512]{2,1,0:T(8,128)(2,1)} custom-call(s32[128]{0:T(128)} %len_hbm.1, bf16[16,576,128]{2,1,0:T(8,128)(2,1)} %bitcast.2, bf16[128,4,1,576,256]{4,3,2,1,0:T(8,128)(2,1)} %bitcast.1.cache_ref), custom_call_target="tpu_custom_call" | custom-call | tf_op jit(solution)/shard_map/pallas_call | solution.py:359
  222.3 3.1 %copy.5 = bf16[16,128,512]{2,1,0:T(8,128)(2,1)} copy(bf16[16,128,512]{2,1,0:T(8,128)(2,1)} %shard_map.37) | data formatting | bytes 4194304

commit v5 on v4

--- a/solution.py
+++ b/solution.py
@@ -15,8 +15,9 @@
 CACHE_SLOTS = 4
 RING = 4
 AG_RING = 8
-LEAD = 1
-FINAL_LAG = 1
+RX_RING = 8
+LEAD = 2
+FINAL_LAG = 2
 
 
 def _kernel(dims, len_hbm, q_hbm, cache_ref, out_ref, len_ref, q_own, q_all, cbuf, o_tx, lse_acc, lse_a, lse_b, rx_d, rx_f, rx_la, rx_lb,
@@ -124,32 +125,32 @@
 
     def d_copy(it, t):
         ring = it % RING
-        return remote(o_tx.at[ring, D0 + t], rx_d.at[it, core], d_send.at[ring], d_recv.at[ring], (x0, y1)[t])
+        return remote(o_tx.at[ring, D0 + t], rx_d.at[it, core], d_send.at[ring], d_recv.at[it % RX_RING], (x0, y1)[t])
 
     def pm_copy(it):
         ring, i = it % RING, it - LEAD
-        return remote(o_tx.at[ring, PM], rx_d.at[i, 2], f_send.at[ring], d_recv.at[i % RING], partner)
+        return remote(o_tx.at[ring, PM], rx_d.at[i, 2], f_send.at[ring], d_recv.at[i % RX_RING], partner)
 
     def f_copy(it, t):
         ring, i = it % RING, it - LEAD
-        return remote(o_tx.at[ring, (F0, F1, PF)[t]], rx_f.at[i, core if t < 2 else 2], f_send.at[ring], f_recv.at[ring],
+        return remote(o_tx.at[ring, (F0, F1, PF)[t]], rx_f.at[i, core if t < 2 else 2], f_send.at[ring], f_recv.at[it % RX_RING],
                       (x0, y1, partner)[t])
 
     def la_copy(it):
         ring, i = it % RING, it - LEAD
-        return remote(lse_a.at[ring], rx_la.at[i], la_send.at[ring], la_recv.at[ring], partner)
+        return remote(lse_a.at[ring], rx_la.at[i], la_send.at[ring], la_recv.at[it % RX_RING], partner)
 
     def lb_copy(it, t):
         ring = it % RING
-        return remote(lse_b.at[ring, t], rx_lb.at[it, core if t < 2 else 2], lb_send.at[ring], lb_recv.at[ring], (x0, y1, partner)[t])
+        return remote(lse_b.at[ring, t], rx_lb.at[it, core if t < 2 else 2], lb_send.at[ring], lb_recv.at[it % RX_RING], (x0, y1, partner)[t])
 
     def m_copy(it):
         ring, i = it % RING, it - LEAD
-        return remote(m_tx.at[ring], rx_m.at[i], m_send.at[ring], m_recv.at[ring], n1)
+        return remote(m_tx.at[ring], rx_m.at[i], m_send.at[ring], m_recv.at[it % RX_RING], n1)
 
     def ml_copy(it):
         ring, i = it % RING, it - LEAD
-        return remote(m_lse.at[ring], rx_ml.at[i], ml_send.at[ring], ml_recv.at[ring], n1)
+        return remote(m_lse.at[ring], rx_ml.at[i], ml_send.at[ring], ml_recv.at[it % RX_RING], n1)
 
     def wait_bytes(ref, sem):
         pltpu.make_async_copy(ref, ref, sem).wait()
@@ -212,9 +213,9 @@
 
     def merge(it):
         ring, i = it % RING, it - LEAD
-        wait_bytes(rx_d.at[i], d_recv.at[i % RING])
-        wait_bytes(rx_lb.at[i], lb_recv.at[i % RING])
-        wait_bytes(rx_la.at[i], la_recv.at[ring])
+        wait_bytes(rx_d.at[i], d_recv.at[i % RX_RING])
+        wait_bytes(rx_lb.at[i], lb_recv.at[i % RX_RING])
+        wait_bytes(rx_la.at[i], la_recv.at[it % RX_RING])
         rows = [lse_a[ring][0:1], rx_lb[i, 0][0:1], rx_lb[i, 1][0:1], rx_la[i][1:2]]
         lse, acc = weighted(rows, [o_tx[ring, OM], rx_d[i, 0], rx_d[i, 1], rx_d[i, 2]])
         m_tx[ring] = acc
@@ -222,14 +223,14 @@
 
     def final(it):
         ring, i = it % RING, it - LEAD
-        wait_bytes(rx_f.at[i], f_recv.at[ring])
+        wait_bytes(rx_f.at[i], f_recv.at[it % RX_RING])
 
         @pl.when(it >= steps)
         def _():
-            wait_bytes(rx_lb.at[it], lb_recv.at[ring])
-
-        wait_bytes(rx_m.at[i], m_recv.at[ring])
-        wait_bytes(rx_ml.at[i], ml_recv.at[ring])
+            wait_bytes(rx_lb.at[it], lb_recv.at[it % RX_RING])
+
+        wait_bytes(rx_m.at[i], m_recv.at[it % RX_RING])
+        wait_bytes(rx_ml.at[i], ml_recv.at[it % RX_RING])
         rows = [lse_b[ring, 2][1:2], rx_lb[it, 0][1:2], rx_lb[it, 1][1:2], rx_lb[it, 2][0:1], rx_ml[i]]
         _, acc = weighted(rows, [o_tx[ring, OF], rx_f[i, 0], rx_f[i, 1], rx_f[i, 2], rx_m[i]])
         o_stage[i % 2] = acc.astype(jnp.bfloat16)
@@ -250,10 +251,9 @@
     ag_own(1)
     ag_forward(0)
     ag_own(2)
+    ag_own(3)
     ag_forward(1)
     ag_relay(0)
-    ag_own(3)
-    ag_relay(1)
     len_load().wait()
 
     def gather(it, phase):
@@ -271,6 +271,9 @@
             @pl.when((it >= 1) & (it < steps // 2))
             def _():
                 ag_relay(2 * it)
+
+            @pl.when(it < steps // 2)
+            def _():
                 ag_relay(2 * it + 1)
 
     @pl.loop(0, steps + LEAD + FINAL_LAG)
@@ -345,6 +348,20 @@
         out_copy(i).wait()
 
 
+def _hand_over(src, dst, buf, in_sem, out_sem):
+    rows = src.shape[0] // 4
+    parts = [pl.ds(k * rows, rows) for k in range(4)]
+    loads = [pltpu.make_async_copy(src.at[p], buf.at[p], in_sem.at[k]) for k, p in enumerate(parts)]
+    stores = [pltpu.make_async_copy(buf.at[p], dst.at[p], out_sem.at[k]) for k, p in enumerate(parts)]
+    for load in loads:
+        load.start()
+    for load, store in zip(loads, stores):
+        load.wait()
+        store.start()
+    for store in stores:
+        store.wait()
+
+
 def solution(mesh):
     group = mesh.shape['dcp']
 
@@ -356,7 +373,7 @@
         latent = width - ROPE_DIM
         bf16, f32 = jnp.bfloat16, jnp.float32
         dma = pltpu.SemaphoreType.DMA
-        return pl.pallas_call(
+        merged = pl.pallas_call(
             functools.partial(_kernel, (steps, group, heads, latent, pages, page_len)),
             out_shape=jax.ShapeDtypeStruct((steps, heads, latent), bf16),
             in_specs=[pl.BlockSpec(memory_space=pl.ANY)] * 3,
@@ -382,10 +399,14 @@
                 pltpu.VMEM((2, heads, latent), bf16),
                 dma, dma, dma((CACHE_SLOTS,)), dma((2,)),
                 dma((7,)), dma((AG_RING, 3)), dma((steps,)),
-                *[dma((RING,))] * 12,
+                *[dma((RING,))] * 6, *[dma((RX_RING,))] * 6,
             ],
             compiler_params=pltpu.CompilerParams(collective_id=0, has_side_effects=True, vmem_limit_bytes=66_000_000),
         )(len_blk, jnp.transpose(q_blk, (1, 2, 0)), jnp.swapaxes(cache_blk, 3, 4))
+        return pl.pallas_call(
+            _hand_over, out_shape=jax.ShapeDtypeStruct((steps, heads, latent), bf16),
+            in_specs=[pl.BlockSpec(memory_space=pl.ANY)], out_specs=pl.BlockSpec(memory_space=pl.ANY),
+            scratch_shapes=[pltpu.VMEM((steps, heads, latent), bf16), dma((4,)), dma((4,))])(merged)
 
     return jax.shard_map(local_step, mesh=mesh, in_specs=(P('dp', 'dcp', None), P('dp', None, 'dcp', None, None), P('dp')),
                          out_specs=P(('dp', 'dcp'), None, None), check_vma=False)

time: 226 us -> 224 us (level)
  local copies, waits for them, and re-layouts: 3.1 us -> 0 us
    unnamed x1 -> x0, local copies, waits for them, and re-layouts: 3.1 us -> none
    pallas_call x0 -> x1, Pallas kernels: none -> 2.42 us  [local_step(): pl.pallas_call(_hand_over, out_shape=jax.ShapeDtypeStruct((steps, heads,...]
where the time goes in v5:
time: 224 us; the launch traced here: 223 us
  Pallas kernels  223 us (100%)
    pallas_call x1, Pallas kernels, local_step(): pl.pallas_call(functools.partial(_kernel, (steps, group, heads, latent, p...  221 us

profile of v5, /device:TPU:0, one launch (start us, length us, event | category | flops | bytes accessed | tf_op | source)
XLA Modules:
  0.0 223.3 jit_solution(2083879117599397305)
XLA Ops:
  0.0 220.9 %shard_map.37.src = bf16[16,128,512]{2,1,0:T(8,128)(2,1)} custom-call(s32[128]{0:T(128)} %len_hbm.1, bf16[16,576,128]{2,1,0:T(8,128)(2,1)} %bitcast.2, bf16[128,4,1,576,256]{4,3,2,1,0:T(8,128)(2,1)} %bitcast.1.cache_ref), custom_call_target="tpu_custom_call" | custom-call | tf_op jit(solution)/shard_map/pallas_call | solution.py:376
  220.9 2.4 %shard_map.38 = bf16[16,128,512]{2,1,0:T(8,128)(2,1)} custom-call(bf16[16,128,512]{2,1,0:T(8,128)(2,1)} %shard_map.37.src), custom_call_target="tpu_custom_call" | custom-call | tf_op jit(solution)/shard_map/pallas_call | solution.py:406

commit v6 on v5

--- a/solution.py
+++ b/solution.py
@@ -16,12 +16,14 @@
 RING = 4
 AG_RING = 8
 RX_RING = 8
+VMEM_BYTES = 54_000_000
+Q_PART = 4
 LEAD = 2
 FINAL_LAG = 2
 
 
 def _kernel(dims, len_hbm, q_hbm, cache_ref, out_ref, len_ref, q_own, q_all, cbuf, o_tx, lse_acc, lse_a, lse_b, rx_d, rx_f, rx_la, rx_lb,
-            m_tx, m_lse, rx_m, rx_ml, w_rows, o_stage, len_sem, q_sem, c_sem, out_sem, ag_send, ag_recv, ag_part,
+            m_tx, m_lse, rx_m, rx_ml, w_rows, len_sem, q_sem, c_sem, ag_send, ag_recv, ag_part,
             d_send, f_send, la_send, lb_send, m_send, ml_send, d_recv, f_recv, la_recv, lb_recv, m_recv, ml_recv):
     steps, group, heads, latent, pages, page_len = dims
     scale = QK_DIM ** -0.5
@@ -62,8 +64,9 @@
     def len_load():
         return pltpu.make_async_copy(len_hbm, len_ref, len_sem)
 
-    def q_load():
-        return pltpu.make_async_copy(q_hbm, q_own, q_sem)
+    def q_load(part):
+        some = pl.ds(part * Q_PART, Q_PART)
+        return pltpu.make_async_copy(q_hbm.at[some], q_own.at[some], q_sem.at[part])
 
     def row(it, p):
         return it if p in (D0, D1) else it - LEAD
@@ -74,9 +77,6 @@
     def c_load(it, p):
         slot = p % CACHE_SLOTS
         return pltpu.make_async_copy(cache_ref.at[owners[p] * steps + row(it, p), :, 0], cbuf.at[slot], c_sem.at[slot])
-
-    def out_copy(i):
-        return pltpu.make_async_copy(o_stage.at[i % 2], out_ref.at[i], out_sem.at[i % 2])
 
     def ag(u, kind):
         block = (me, me, me, n2, n2, n1, diag)[kind]
@@ -89,10 +89,12 @@
     own_heads = heads // group
     own_head = wide_row % own_heads
 
-    def q_build(u):
+    def q_build(u, loading=False):
         chosen = wide_lane == wide_row // own_heads * steps + u
         acc = None
         for h in range(0, own_heads, 2):
+            if loading and h % Q_PART == 0:
+                q_load(h // Q_PART).wait()
             one_hot = jnp.concatenate([jnp.where(chosen & (own_head == g), 1.0, 0.0) for g in (h, h + 1)], axis=1)
             pair = jnp.concatenate([q_own[h], q_own[h + 1]], axis=1)
             term = lax.dot_general(one_hot.astype(jnp.bfloat16), pair, (((1,), (1,)), ((), ())), preferred_element_type=jnp.float32)
@@ -233,21 +235,21 @@
         wait_bytes(rx_ml.at[i], ml_recv.at[it % RX_RING])
         rows = [lse_b[ring, 2][1:2], rx_lb[it, 0][1:2], rx_lb[it, 1][1:2], rx_lb[it, 2][0:1], rx_ml[i]]
         _, acc = weighted(rows, [o_tx[ring, OF], rx_f[i, 0], rx_f[i, 1], rx_f[i, 2], rx_m[i]])
-        o_stage[i % 2] = acc.astype(jnp.bfloat16)
-
-    q_load().start()
+        out_ref[i] = acc.astype(jnp.bfloat16)
+
+    for part in range(own_heads // Q_PART):
+        q_load(part).start()
+
+    w_rows[...] = jnp.zeros_like(w_rows)
+    lse_acc[...] = jnp.zeros_like(lse_acc)
+    q_build(0, loading=True)
+    pl.semaphore_wait(barrier, len(peers))
+
+    ag_send_own(0)
     len_load().start()
     for p in range(CACHE_SLOTS - 1):
         if p in (D0, D1):
             c_load(0, p).start()
-
-    w_rows[...] = jnp.zeros_like(w_rows)
-    lse_acc[...] = jnp.zeros_like(lse_acc)
-    q_load().wait()
-    q_build(0)
-    pl.semaphore_wait(barrier, len(peers))
-
-    ag_send_own(0)
     ag_own(1)
     ag_forward(0)
     ag_own(2)
@@ -330,12 +332,7 @@
         def _():
             k = it - FINAL_LAG
 
-            @pl.when(k >= LEAD + 2)
-            def _():
-                out_copy(k - LEAD - 2).wait()
-
             final(k)
-            out_copy(k - LEAD).start()
 
     @pl.loop(steps + LEAD + FINAL_LAG - RING, steps + LEAD)
     def _(it):
@@ -343,23 +340,6 @@
 
     for kind in range(7):
         wait_bytes(q_all.at[:, :, kind], ag_send.at[kind])
-
-    for i in (steps - 2, steps - 1):
-        out_copy(i).wait()
-
-
-def _hand_over(src, dst, buf, in_sem, out_sem):
-    rows = src.shape[0] // 4
-    parts = [pl.ds(k * rows, rows) for k in range(4)]
-    loads = [pltpu.make_async_copy(src.at[p], buf.at[p], in_sem.at[k]) for k, p in enumerate(parts)]
-    stores = [pltpu.make_async_copy(buf.at[p], dst.at[p], out_sem.at[k]) for k, p in enumerate(parts)]
-    for load in loads:
-        load.start()
-    for load, store in zip(loads, stores):
-        load.wait()
-        store.start()
-    for store in stores:
-        store.wait()
 
 
 def solution(mesh):
@@ -373,11 +353,11 @@
         latent = width - ROPE_DIM
         bf16, f32 = jnp.bfloat16, jnp.float32
         dma = pltpu.SemaphoreType.DMA
-        merged = pl.pallas_call(
+        return pl.pallas_call(
             functools.partial(_kernel, (steps, group, heads, latent, pages, page_len)),
             out_shape=jax.ShapeDtypeStruct((steps, heads, latent), bf16),
-            in_specs=[pl.BlockSpec(memory_space=pl.ANY)] * 3,
-            out_specs=pl.BlockSpec(memory_space=pl.ANY),
+            in_specs=[pl.BlockSpec(memory_space=pltpu.HBM)] * 3,
+            out_specs=pl.BlockSpec(memory_space=pltpu.VMEM),
             scratch_shapes=[
                 pltpu.SMEM((batch,), jnp.int32),
                 pltpu.VMEM((own_heads, width, batch), bf16),
@@ -396,17 +376,12 @@
                 pltpu.VMEM((steps, heads, latent), f32),
                 pltpu.VMEM((steps, 1, heads), f32),
                 pltpu.VMEM((128, heads), f32),
-                pltpu.VMEM((2, heads, latent), bf16),
-                dma, dma, dma((CACHE_SLOTS,)), dma((2,)),
+                dma, dma((own_heads // Q_PART,)), dma((CACHE_SLOTS,)),
                 dma((7,)), dma((AG_RING, 3)), dma((steps,)),
                 *[dma((RING,))] * 6, *[dma((RX_RING,))] * 6,
             ],
-            compiler_params=pltpu.CompilerParams(collective_id=0, has_side_effects=True, vmem_limit_bytes=66_000_000),
+            compiler_params=pltpu.CompilerParams(collective_id=0, has_side_effects=True, vmem_limit_bytes=VMEM_BYTES),
         )(len_blk, jnp.transpose(q_blk, (1, 2, 0)), jnp.swapaxes(cache_blk, 3, 4))
-        return pl.pallas_call(
-            _hand_over, out_shape=jax.ShapeDtypeStruct((steps, heads, latent), bf16),
-            in_specs=[pl.BlockSpec(memory_space=pl.ANY)], out_specs=pl.BlockSpec(memory_space=pl.ANY),
-            scratch_shapes=[pltpu.VMEM((steps, heads, latent), bf16), dma((4,)), dma((4,))])(merged)
 
     return jax.shard_map(local_step, mesh=mesh, in_specs=(P('dp', 'dcp', None), P('dp', None, 'dcp', None, None), P('dp')),
                          out_specs=P(('dp', 'dcp'), None, None), check_vma=False)

time: 224 us -> 222 us (level)
  Pallas kernels: 223 us -> 220 us
    pallas_call x1 -> x0, Pallas kernels: 2.42 us -> none  [local_step(): pl.pallas_call(_hand_over, out_shape=jax.ShapeDtypeStruct((steps, heads,...]
where the time goes in v6:
time: 222 us
  Pallas kernels  220 us (99%)
    pallas_call x1, Pallas kernels, local_step(): pl.pallas_call(functools.partial(_kernel, (steps, group, heads, latent, p...  220 us

profile of v6, /device:TPU:0, one launch (start us, length us, event | category | flops | bytes accessed | tf_op | source)
XLA Modules:
  0.0 221.7 jit_solution(17973864683865567508)
XLA Ops:
  0.0 0.0 copy-start
  0.0 0.7 copy-done
  0.7 219.8 %shard_map.37 = bf16[16,128,512]{2,1,0:T(8,128)(2,1)S(1)} custom-call(s32[128]{0:T(128)S(1)} %copy-done, bf16[16,576,128]{2,1,0:T(8,128)(2,1)} %bitcast.2, bf16[128,4,1,576,256]{4,3,2,1,0:T(8,128)(2,1)} %bitcast.1.cache_ref), custom_call_target="tpu_custom_call" | custom-call | tf_op jit(solution)/shard_map/pallas_call | solution.py:356
  220.4 1.3 copy.5
Async XLA Ops:
  0.0 0.7 copy-start

commit v7 on v6

--- a/solution.py
+++ b/solution.py
@@ -381,7 +381,7 @@
                 *[dma((RING,))] * 6, *[dma((RX_RING,))] * 6,
             ],
             compiler_params=pltpu.CompilerParams(collective_id=0, has_side_effects=True, vmem_limit_bytes=VMEM_BYTES),
-        )(len_blk, jnp.transpose(q_blk, (1, 2, 0)), jnp.swapaxes(cache_blk, 3, 4))
+        )(pltpu.with_memory_space_constraint(len_blk, pltpu.HBM), jnp.transpose(q_blk, (1, 2, 0)), jnp.swapaxes(cache_blk, 3, 4))
 
     return jax.shard_map(local_step, mesh=mesh, in_specs=(P('dp', 'dcp', None), P('dp', None, 'dcp', None, None), P('dp')),
                          out_specs=P(('dp', 'dcp'), None, None), check_vma=False)

time: 222 us -> 221 us (level)
  no operation moved by 1% of the time
where the time goes in v7:
time: 221 us
  Pallas kernels  220 us (100%)
    pallas_call x1, Pallas kernels, local_step(): pl.pallas_call(functools.partial(_kernel, (steps, group, heads, latent, p...  220 us

profile of v7, /device:TPU:0, one launch (start us, length us, event | category | flops | bytes accessed | tf_op | source)
XLA Modules:
  0.0 221.1 jit_solution(13863772668538073394)
XLA Ops:
  0.0 219.8 %shard_map.37 = bf16[16,128,512]{2,1,0:T(8,128)(2,1)S(1)} custom-call(s32[128]{0:T(128)} %len_hbm.1, bf16[16,576,128]{2,1,0:T(8,128)(2,1)} %bitcast.2, bf16[128,4,1,576,256]{4,3,2,1,0:T(8,128)(2,1)} %bitcast.1.cache_ref), custom_call_target="tpu_custom_call" | custom-call | tf_op jit(solution)/shard_map/pallas_call | solution.py:356
  219.8 1.3 copy.5
